TPU v7x, 32 devices: a whole 2x2x4 slice. The times are simulated.
32 devices in a mesh: gx: 4 (over z), gy: 2 (over y), gz: 4 (over x, core).
Axes of the slice: x: 2, y: 2, z: 4, core: 2. Of those that a mesh axis runs over, the one named last changes fastest.
Arguments:
- tokens: bfloat16 [32768, 4096], P(('gx', 'gy', 'gz')), may hold values from -300 to 300
- cotangents: bfloat16 [32768, 1024], P(('gx', 'gy', 'gz')), may hold values from -17 to 17
- master: float32 [4096, 1024], P(('gx', 'gy', 'gz')), may hold values from -0.09375 to 0.09375
- first_moment: float32 [4096, 1024], P(('gx', 'gy', 'gz')), may hold values from -6 to 6
- second_moment: float32 [4096, 1024], P(('gx', 'gy', 'gz')), may hold values from 0.1 to 10
Outputs:
- weights: bfloat16 [4096, 1024], replicated
- new_master: float32 [4096, 1024], P(('gx', 'gy', 'gz'))
- new_first: float32 [4096, 1024], P(('gx', 'gy', 'gz'))
- new_second: float32 [4096, 1024], P(('gx', 'gy', 'gz'))
All inputs are finite; a program needn't handle non-finite values.
Results may differ from a plain program's by a relative error of at most 0.002.
Values may be sent and summed in bfloat16 or wider, within the bound.
A program may use at most 128 MiB of HBM per device.

v0:
```python
import jax
import jax.numpy as jnp
from jax import lax
from jax.sharding import PartitionSpec as P

ADAM_STEP = 10


beta_first = 0.9
beta_second = 0.95
learn_rate = 0.001
decay_rate = 0.1
epsilon = 1e-08


def shards(tokens, cotangents, master, first_moment, second_moment):
    width = tokens.shape[1]
    columns = cotangents.shape[1]
    gradient = lax.psum_scatter(
        lax.dot_general(
            tokens, cotangents, (((0,), (0,)), ((), ())), preferred_element_type=jnp.float32
        ),
        ("gx", "gy", "gz"),
        scatter_dimension=0,
        tiled=True,
    )
    squares = lax.psum(jnp.sum(gradient * gradient), ("gx", "gy", "gz"))
    grad_norm = jnp.sqrt(squares)
    clip_norm = jnp.sqrt(jnp.float32(width * columns))
    factor = clip_norm / jnp.maximum(grad_norm, clip_norm)
    clipped = factor * gradient
    new_first = beta_first * first_moment + (1.0 - beta_first) * clipped
    new_second = beta_second * second_moment + (1.0 - beta_second) * clipped * clipped
    first_hat = new_first / (1.0 - beta_first**ADAM_STEP)
    second_hat = new_second / (1.0 - beta_second**ADAM_STEP)
    new_master = master - learn_rate * (
        first_hat / (jnp.sqrt(second_hat) + epsilon) + decay_rate * master
    )
    updated = new_master.astype(jnp.bfloat16)
    gathered = lax.all_gather(updated, ("gx", "gy", "gz"), axis=0, tiled=True)
    return (gathered, new_master, new_first, new_second)


def solution(mesh):
    return jax.shard_map(
        shards,
        mesh=mesh,
        in_specs=(
            P(("gx", "gy", "gz"), None),
            P(("gx", "gy", "gz"), None),
            P(("gx", "gy", "gz"), None),
            P(("gx", "gy", "gz"), None),
            P(("gx", "gy", "gz"), None),
        ),
        out_specs=(
            P(),
            P(("gx", "gy", "gz"), None),
            P(("gx", "gy", "gz"), None),
            P(("gx", "gy", "gz"), None),
        ),
        check_vma=False,
    )
```

profile of v0, /device:TPU:9, one launch (start us, length us, event | category | flops | bytes accessed | tf_op | source)
XLA Modules:
  0.0 346.3 jit_solution(4435537236314636996)
XLA Ops:
  7.2 0.0 copy-start
  7.2 0.0 reduce-scatter.2.cloned.1.call-start
  7.2 1.5 copy-done
  8.8 14.6 %fusion.3 = f32[4096,1024]{1,0:T(8,128)} fusion(bf16[1024,4096]{1,0:T(8,128)(2,1)} %param.5, bf16[1024,1024]{1,0:T(8,128)(2,1)S(1)} %copy-done), kind=kOutput, calls=%fused_computation.6 | convolution fusion | flops 8589934592 | bytes 27262976 | tf_op jit(solution)/shard_map/dot_general | solution.py:20
  23.3 0.0 copy-start.1
  23.3 0.0 copy-start.2
  23.3 0.0 reduce-scatter.2.cloned.1.call-update
  23.3 0.0 all-gather.2.cloned.1.call-start
  23.4 184.5 %reduce-scatter.2.cloned.1.call-done = f32[128,1024]{1,0:T(8,128)} async-done(((f32[4096,1024]{1,0:T(8,128)}), f32[128,1024]{1,0:T(8,128)}) %reduce-scatter.2.cloned.1.call-update) | async-done | bytes 524304 | tf_op jit(solution)/shard_map/reduce_scatter | solution.py:19
  207.9 1.8 multiply_reduce_fusion
  209.7 40.2 %psum.7 = f32[]{:T(128)} all-reduce(f32[]{:T(128)} %multiply_reduce_fusion), channel_id=1, replica_groups=mesh['gx'=4,'gy'=2,'gz'=4] {'gx','gy','gz'}, use_global_device_ids=true, to_apply=%region_2.0 | all-reduce | flops 1 | bytes 8 | tf_op jit(solution)/shard_map/psum | solution.py:27
  250.6 0.0 copy-done.1
  250.7 0.0 copy-done.2
  250.7 2.7 fusion.1
  253.4 0.0 all-gather.2.cloned.1.call-update
  253.4 78.2 %all-gather.2.cloned.1.call-done = bf16[4096,1024]{1,0:T(8,128)(2,1)} async-done(((bf16[128,1024]{1,0:T(8,128)(2,1)}), bf16[4096,1024]{1,0:T(8,128)(2,1)}) %all-gather.2.cloned.1.call-update) | async-done | bytes 8388624 | tf_op jit(solution)/shard_map/all_gather | solution.py:40
  331.7 7.8 %copy.10 = bf16[4096,1024]{1,0:T(8,128)(2,1)} copy(bf16[4096,1024]{1,0:T(8,128)(2,1)} %all-gather.2.cloned.1.call-done) | data formatting | bytes 16777216
Async XLA Ops:
  7.2 1.6 copy-start
  7.2 200.7 %reduce-scatter.2.cloned.1.call-start = ((), (), s32[]{:S(2)}) async-start(), calls=%async_computation.1 | async-start | bytes 17301504 | tf_op jit(solution)/shard_map/reduce_scatter | solution.py:19
  23.3 227.3 %copy-start.1 = (f32[128,1024]{1,0:T(8,128)S(1)}, f32[128,1024]{1,0:T(8,128)}, u32[]{:S(2)}) copy-start(f32[128,1024]{1,0:T(8,128)} %param.7) | copy-start | bytes 1572868
  23.3 227.3 %copy-start.2 = (f32[128,1024]{1,0:T(8,128)S(1)}, f32[128,1024]{1,0:T(8,128)}, u32[]{:S(2)}) copy-start(f32[128,1024]{1,0:T(8,128)} %param.8) | copy-start | bytes 1572868
  23.3 308.3 %all-gather.2.cloned.1.call-start = ((), (), s32[]{:S(2)}) async-start(), calls=%async_computation.2 | async-start | bytes 8650752 | tf_op jit(solution)/shard_map/all_gather | solution.py:40
Sparse Core Ops, SparseCore 0:
  23.5 184.3 reduce-scatter.1
  253.5 78.0 all-gather.1
where the time goes:
time: 348 us; the launch traced here: 346 us
  waiting for transfers between devices  263 us (76%)
  blocking collectives  40.2 us (12%)
  between operations  14.8 us (4%)
  matrix products  14.6 us (4%)
  local copies, waits for them, and re-layouts  9.31 us (3%)
  other arithmetic  4.5 us (1%)
    reduce_scatter x1, waiting for transfers between devices, shards(): lax.psum_scatter(lax.dot_general(tokens, cotangents, (((0,), (0,)), ((),...  184 us
    all_gather x1, waiting for transfers between devices, shards(): gathered = lax.all_gather(updated, ('gx', 'gy', 'gz'), axis=0, tiled=True)  78.2 us
    psum x1, blocking collectives, shards(): squares = lax.psum(jnp.sum(gradient * gradient), ('gx', 'gy', 'gz'))  40.2 us
    dot_general x1, matrix products, shards(): lax.dot_general(tokens, cotangents, (((0,), (0,)), ((), ())), preferred_e...  14.6 us
    unnamed x7, local copies, waits for them, and re-layouts  9.31 us
  transfers between devices with their start and end apart: 2, of which 2 were waited for; matrix products, arithmetic and copies ran while one was open for 0% of the time, Pallas kernels for 0%

commit v1 on v0

v1 whole, which is shorter than its diff:
```python
import functools
import math

import jax
import jax.numpy as jnp
from jax import lax
from jax.experimental import pallas as pl
from jax.experimental.pallas import tpu as pltpu
from jax.sharding import PartitionSpec as P

ADAM_STEP = 10
beta_first = 0.9
beta_second = 0.95
learn_rate = 0.001
decay_rate = 0.1
epsilon = 1e-08

AXES = ("gx", "gy", "gz")
LANES = 128
MESH = pl.DeviceIdType.MESH


class Copies:
    def __init__(self, send_sem=None, recv_sem=None):
        self.send_sem, self.recv_sem = send_sem, recv_sem
        self.made = []

    def start(self, src, dst, device):
        at = len(self.made)
        copy = pltpu.make_async_remote_copy(
            src_ref=src,
            dst_ref=dst,
            send_sem=self.send_sem.at[at],
            recv_sem=self.recv_sem.at[at],
            device_id=device,
            device_id_type=MESH,
        )
        copy.start()
        self.made.append(copy)
        return copy


def kernel(
    sizes, chunks, clip_norm,
    part, master, first, second,
    weights, new_master, new_first, new_second,
    recv0, send1p, recv1p, send1q, recv1q, send2p, recv2p, send2q, recv2q, send3, recv3,
    grad, squares, full, send_sem, recv_sem, out_sem,
):
    gx, gy, gxx = sizes
    rows = part.shape[4]
    f32, bf16 = jnp.float32, jnp.bfloat16
    z, y, g = lax.axis_index("gx"), lax.axis_index("gy"), lax.axis_index("gz")
    x, core = g // 2, g % 2
    other = 1 - core
    gz = 2 * gxx

    def along_z(o):
        return {"gx": lax.rem(z + o, gx)}

    def along_y(o):
        return {"gy": lax.rem(y + o, gy)}

    def along_x(o):
        return {"gz": lax.rem(x + o, gxx) * 2 + core}

    partner = {"gz": x * 2 + other}

    barrier = pltpu.get_barrier_semaphore()
    for o in range(1, gz):
        pl.semaphore_signal(barrier, inc=1, device_id={"gz": lax.rem(g + o, gz)}, device_id_type=MESH)
    for o in range(1, gy):
        pl.semaphore_signal(barrier, inc=1, device_id=along_y(o), device_id_type=MESH)
    for o in range(1, gx):
        pl.semaphore_signal(barrier, inc=1, device_id=along_z(o), device_id_type=MESH)
    pl.semaphore_wait(barrier, gz + gy + gx - 3)

    copies = Copies(send_sem, recv_sem)
    width = 2 * LANES

    def cols(k):
        return pl.ds(k * width, width)

    def colp(k):
        return pl.ds(k * width, LANES)

    def colq(k):
        return pl.ds(k * width + LANES, LANES)

    lane_p, lane_q = pl.ds(0, LANES), pl.ds(LANES, LANES)

    core_in = [
        copies.start(part.at[:, :, :, other, :, cols(k)], recv0.at[k], partner)
        for k in range(chunks)
    ]

    def pair(k, i, j, l, col, lane):
        return part[i, j, l, core, :, col].astype(f32) + recv0[k, i, j, l, :, lane].astype(f32)

    first_p, first_q, second_p, second_q, third = {}, {}, {}, {}, {}

    def stage1(k):
        core_in[k].wait_recv()
        first_p[k], first_q[k] = [], []
        for o in range(1, gxx):
            xp = lax.rem(x + o, gxx)

            def body(i, _):
                for j in range(gy):
                    send1p[k, o - 1, i, j] = pair(k, i, j, xp, colp(k), lane_p).astype(bf16)
                return 0

            lax.fori_loop(0, gx, body, 0)
            first_p[k].append(copies.start(send1p.at[k, o - 1], recv1p.at[k, o - 1], along_x(o)))
        for o in range(1, gy):
            yp = lax.rem(y + o, gy)

            def body(i, _):
                for l in range(gxx):
                    send1q[k, o - 1, i, l] = pair(k, i, yp, l, colq(k), lane_q).astype(bf16)
                return 0

            lax.fori_loop(0, gx, body, 0)
            first_q[k].append(copies.start(send1q.at[k, o - 1], recv1q.at[k, o - 1], along_y(o)))

    def after_p(k, i, j):
        total = pair(k, i, j, x, colp(k), lane_p)
        for o in range(1, gxx):
            total += recv1p[k, o - 1, i, j].astype(f32)
        return total

    def after_q(k, i, l):
        total = pair(k, i, y, l, colq(k), lane_q)
        for o in range(1, gy):
            total += recv1q[k, o - 1, i, l].astype(f32)
        return total

    def stage2(k):
        second_p[k], second_q[k] = [], []
        for copy in first_p[k]:
            copy.wait_recv()
        for o in range(1, gy):
            yp = lax.rem(y + o, gy)

            def body(i, _):
                send2p[k, o - 1, i] = after_p(k, i, yp).astype(bf16)
                return 0

            lax.fori_loop(0, gx, body, 0)
            second_p[k].append(copies.start(send2p.at[k, o - 1], recv2p.at[k, o - 1], along_y(o)))
        for copy in first_q[k]:
            copy.wait_recv()
        for o in range(1, gxx):
            xp = lax.rem(x + o, gxx)

            def body(i, _):
                send2q[k, o - 1, i] = after_q(k, i, xp).astype(bf16)
                return 0

            lax.fori_loop(0, gx, body, 0)
            second_q[k].append(copies.start(send2q.at[k, o - 1], recv2q.at[k, o - 1], along_x(o)))

    def plane_p(k, i):
        total = after_p(k, i, y)
        for o in range(1, gy):
            total += recv2p[k, o - 1, i].astype(f32)
        return total

    def plane_q(k, i):
        total = after_q(k, i, x)
        for o in range(1, gxx):
            total += recv2q[k, o - 1, i].astype(f32)
        return total

    def stage3(k):
        for copy in second_p[k] + second_q[k]:
            copy.wait_recv()
        third[k] = []
        for o in range(1, gx):
            zp = lax.rem(z + o, gx)
            send3[k, o - 1, :, lane_p] = plane_p(k, zp).astype(bf16)
            send3[k, o - 1, :, lane_q] = plane_q(k, zp).astype(bf16)
            third[k].append(copies.start(send3.at[k, o - 1], recv3.at[k, o - 1], along_z(o)))

    def stage4(k):
        for copy in third[k]:
            copy.wait_recv()
        total = jnp.zeros((8, LANES), f32)
        for lane, col, plane in ((lane_p, colp(k), plane_p), (lane_q, colq(k), plane_q)):
            value = plane(k, z)
            for o in range(1, gx):
                value += recv3[k, o - 1, :, lane].astype(f32)
            grad[:, col] = value
            total += jnp.sum((value * value).reshape(rows // 8, 8, LANES), axis=0)
        return total

    total = jnp.zeros((8, LANES), f32)
    for t in range(chunks + 3):
        if t < chunks:
            stage1(t)
        if 0 <= t - 1 < chunks:
            stage2(t - 1)
        if 0 <= t - 2 < chunks:
            stage3(t - 2)
        if 0 <= t - 3 < chunks:
            total += stage4(t - 3)

    at = 0
    for axis, count in (("gx", gx), ("gy", gy), ("gz", gz)):
        squares[at] = total
        mine = lax.axis_index(axis)
        moved = [
            copies.start(squares.at[at], squares.at[at + o], {axis: lax.rem(mine + o, count)})
            for o in range(1, count)
        ]
        for o, copy in enumerate(moved, 1):
            copy.wait_recv()
            total += squares[at + o]
        at += count
    norm = jnp.sqrt(jnp.broadcast_to(jnp.sum(total, keepdims=True), (8, LANES)))
    factor = (clip_norm / jnp.maximum(norm, clip_norm))[0:1, :]

    fourth = {}

    def update(k):
        for col in (colp(k), colq(k)):
            clipped = factor * grad[:, col]
            m = beta_first * first[:, col] + (1.0 - beta_first) * clipped
            v = beta_second * second[:, col] + (1.0 - beta_second) * clipped * clipped
            new_first[:, col] = m
            new_second[:, col] = v
            first_hat = m / (1.0 - beta_first**ADAM_STEP)
            second_hat = v / (1.0 - beta_second**ADAM_STEP)
            w = master[:, col]
            w = w - learn_rate * (first_hat / (jnp.sqrt(second_hat) + epsilon) + decay_rate * w)
            new_master[:, col] = w
            full[z, y, x, core, :, col] = w.astype(bf16)
        here = full.at[z, y, x, core, :, cols(k)]
        fourth[k] = [copies.start(here, here, along_z(o)) for o in range(1, gx)]

    fifth, sixth, last, stores = {}, {}, {}, []

    def stage5(k):
        for copy in fourth[k]:
            copy.wait_recv()
        p = full.at[:, y, x, core, :, colp(k)]
        q = full.at[:, y, x, core, :, colq(k)]
        fifth[k] = [copies.start(p, p, along_y(o)) for o in range(1, gy)]
        fifth[k] += [copies.start(q, q, along_x(o)) for o in range(1, gxx)]

    def stage6(k):
        for copy in fifth[k]:
            copy.wait_recv()
        p = full.at[:, :, x, core, :, colp(k)]
        q = full.at[:, y, :, core, :, colq(k)]
        sixth[k] = [copies.start(p, p, along_x(o)) for o in range(1, gxx)]
        sixth[k] += [copies.start(q, q, along_y(o)) for o in range(1, gy)]

    def store(k, half, which):
        src = full.at[:, :, :, half, :, cols(k)]
        dst = weights.at[:, :, :, half, :, cols(k)]
        copy = pltpu.make_async_copy(src, dst, out_sem.at[2 * k + which])
        copy.start()
        stores.append(copy)

    def stage7(k):
        for copy in sixth[k]:
            copy.wait_recv()
        half = full.at[:, :, :, core, :, cols(k)]
        last[k] = copies.start(half, half, partner)
        store(k, core, 0)

    def stage8(k):
        last[k].wait_recv()
        store(k, other, 1)

    for k in range(chunks):
        update(k)
    for t in range(chunks + 3):
        if t < chunks:
            stage5(t)
        if 0 <= t - 1 < chunks:
            stage6(t - 1)
        if 0 <= t - 2 < chunks:
            stage7(t - 2)
        if 0 <= t - 3 < chunks:
            stage8(t - 3)
    for copy in copies.made:
        copy.wait_send()
    for copy in stores:
        copy.wait()


def shards(sizes, tokens, cotangents, master, first_moment, second_moment):
    gx, gy, gxx = sizes
    width, columns = tokens.shape[1], cotangents.shape[1]
    rows = master.shape[0]
    chunks = columns // (2 * LANES)
    clip_norm = math.sqrt(width * columns)
    f32, bf16 = jnp.float32, jnp.bfloat16
    partial = lax.dot_general(
        tokens, cotangents, (((0,), (0,)), ((), ())), preferred_element_type=f32
    ).astype(bf16)
    whole = (gx, gy, gxx, 2, rows, columns)
    per_chunk = (1 + 2 * ((gxx - 1) + (gy - 1)) + (gx - 1)) * 2
    count = chunks * per_chunk + gx + gy + 2 * gxx - 3
    block = (rows, LANES)
    vmem = pl.BlockSpec(memory_space=pltpu.VMEM)
    state = jax.ShapeDtypeStruct((rows, columns), f32)

    def twice(*shape):
        return [pltpu.VMEM((chunks,) + shape, bf16)] * 2

    weights, new_master, new_first, new_second = pl.pallas_call(
        functools.partial(kernel, sizes, chunks, clip_norm),
        out_shape=(jax.ShapeDtypeStruct(whole, bf16), state, state, state),
        in_specs=[vmem] * 4,
        out_specs=(pl.BlockSpec(memory_space=pl.ANY), vmem, vmem, vmem),
        scratch_shapes=[
            pltpu.VMEM((chunks, gx, gy, gxx, rows, 2 * LANES), bf16),
            *twice(gxx - 1, gx, gy, *block),
            *twice(gy - 1, gx, gxx, *block),
            *twice(gy - 1, gx, *block),
            *twice(gxx - 1, gx, *block),
            *twice(gx - 1, rows, 2 * LANES),
            pltpu.VMEM((rows, columns), f32),
            pltpu.VMEM((gx + gy + 2 * gxx, 8, LANES), f32),
            pltpu.VMEM(whole, bf16),
            pltpu.SemaphoreType.DMA((count,)),
            pltpu.SemaphoreType.DMA((count,)),
            pltpu.SemaphoreType.DMA((2 * chunks,)),
        ],
        compiler_params=pltpu.CompilerParams(
            collective_id=0, has_side_effects=True, vmem_limit_bytes=48 * 1024 * 1024
        ),
    )(partial.reshape(whole), master, first_moment, second_moment)
    return (weights.reshape(width, columns), new_master, new_first, new_second)


def solution(mesh):
    sizes = (mesh.shape["gx"], mesh.shape["gy"], mesh.shape["gz"] // 2)
    split = P(AXES, None)
    return jax.shard_map(
        functools.partial(shards, sizes),
        mesh=mesh,
        in_specs=(split,) * 5,
        out_specs=(P(), split, split, split),
        check_vma=False,
    )
```

time: 348 us -> 148 us (0.43)
  waiting for transfers between devices: 263 us -> 0 us
  Pallas kernels: 0 us -> 121 us
  blocking collectives: 40.2 us -> 0 us
  between operations: 14.8 us -> 0.68 us
  other arithmetic: 4.5 us -> 0 us
    reduce_scatter x1 -> x0, waiting for transfers between devices: 184 us -> none  [shards(): lax.psum_scatter(lax.dot_general(tokens, cotangents, (((0,), (0,)), ((),...]
    pallas_call x0 -> x1, Pallas kernels: none -> 121 us  [shards(): pl.pallas_call(functools.partial(kernel, sizes, chunks, clip_norm), out_s...]
    all_gather x1 -> x0, waiting for transfers between devices: 78.2 us -> none  [shards(): gathered = lax.all_gather(updated, ('gx', 'gy', 'gz'), axis=0, tiled=True)]
    psum x1 -> x0, blocking collectives: 40.2 us -> none  [shards(): squares = lax.psum(jnp.sum(gradient * gradient), ('gx', 'gy', 'gz'))]
    unnamed x7 -> x12, local copies, waits for them, and re-layouts: 9.31 us -> 11.7 us
  transfers between devices with their start and end apart: 2 -> 0, of which waited for: 2 -> 0; matrix products, arithmetic and copies ran while one was open for 0% -> 0% of each run, Pallas kernels for 0% -> 0%
where the time goes in v1:
time: 148 us
  Pallas kernels  121 us (82%)
  matrix products  14.6 us (10%)
  local copies, waits for them, and re-layouts  11.7 us (8%)
    pallas_call x1, Pallas kernels, shards(): pl.pallas_call(functools.partial(kernel, sizes, chunks, clip_norm), out_s...  121 us
    dot_general x1, matrix products, shards(): lax.dot_general(tokens, cotangents, (((0,), (0,)), ((), ())), preferred_e...  14.6 us
    unnamed x12, local copies, waits for them, and re-layouts  11.7 us

profile of v1, /device:TPU:9, one launch (start us, length us, event | category | flops | bytes accessed | tf_op | source)
XLA Modules:
  0.0 148.0 jit_solution(4764834411916830736)
XLA Ops:
  0.6 0.0 copy-start
  0.6 0.0 copy-start.3
  0.7 0.0 copy-start.2
  0.7 0.0 copy-start.1
  0.7 1.6 %copy-done = bf16[1024,1024]{1,0:T(8,128)(2,1)S(1)} copy-done((bf16[1024,1024]{1,0:T(8,128)(2,1)S(1)}, bf16[1024,1024]{1,0:T(8,128)(2,1)}, u32[]{:S(2)}) %copy-start) | copy-done | bytes 2097176
  2.2 14.6 %convolution_convert_fusion = bf16[4096,1024]{1,0:T(8,128)(2,1)} fusion(bf16[1024,4096]{1,0:T(8,128)(2,1)} %param.5, bf16[1024,1024]{1,0:T(8,128)(2,1)S(1)} %copy-done), kind=kOutput, calls=%fused_computation | convolution fusion | flops 8594128896 | bytes 18874368 | tf_op jit(solution)/shard_map/dot_general | solution.py:301
  16.8 0.0 copy-done.3
  16.8 0.0 copy-done.2
  16.8 0.0 copy-done.1
  16.8 121.0 %shard_map.84 = (bf16[4,2,2,2,128,1024]{5,4,3,2,1,0:T(8,128)(2,1)}, f32[128,1024]{1,0:T(8,128)S(1)}, f32[128,1024]{1,0:T(8,128)S(1)}, f32[128,1024]{1,0:T(8,128)S(1)}) custom-call(bf16[4,2,2,2,128,1024]{5,4,3,2,1,0:T(8,128)(2,1)} %bitcast.4, f32[128,1024]{1,0:T(8,128)S(1)} %copy-done.1, f32[128,1024]{1,0:T(8,128)S(1)} %copy-done.2, f32[128,1024]{1,0:T(8,128)S(1)} %copy-done.3), custom_call_target="tpu_custom_call" | custom-call | tf_op jit(solution)/shard_map/pallas_call | solution.py:314
  137.8 7.8 %copy.13 = bf16[4096,1024]{1,0:T(8,128)(2,1)} copy(bf16[4096,1024]{1,0:T(8,128)(2,1)} %bitcast.5) | data formatting | bytes 16777216
  145.6 0.8 copy.14
  146.4 0.8 copy.15
  147.2 0.8 copy.16
Async XLA Ops:
  0.6 1.6 %copy-start = (bf16[1024,1024]{1,0:T(8,128)(2,1)S(1)}, bf16[1024,1024]{1,0:T(8,128)(2,1)}, u32[]{:S(2)}) copy-start(bf16[1024,1024]{1,0:T(8,128)(2,1)} %param.6) | copy-start | bytes 6291460
  0.6 16.1 %copy-start.3 = (f32[128,1024]{1,0:T(8,128)S(1)}, f32[128,1024]{1,0:T(8,128)}, u32[]{:S(2)}) copy-start(f32[128,1024]{1,0:T(8,128)} %second.1) | copy-start | bytes 1572868
  0.7 16.1 %copy-start.2 = (f32[128,1024]{1,0:T(8,128)S(1)}, f32[128,1024]{1,0:T(8,128)}, u32[]{:S(2)}) copy-start(f32[128,1024]{1,0:T(8,128)} %first.1) | copy-start | bytes 1572868
  0.7 16.1 %copy-start.1 = (f32[128,1024]{1,0:T(8,128)S(1)}, f32[128,1024]{1,0:T(8,128)}, u32[]{:S(2)}) copy-start(f32[128,1024]{1,0:T(8,128)} %master.1) | copy-start | bytes 1572868

commit v2 on v1

--- a/solution.py
+++ b/solution.py
@@ -42,9 +42,9 @@
 
 def kernel(
     sizes, chunks, clip_norm,
-    part, master, first, second,
+    tokens, cotangents, master, first, second,
     weights, new_master, new_first, new_second,
-    recv0, send1p, recv1p, send1q, recv1q, send2p, recv2p, send2q, recv2q, send3, recv3,
+    flipped, part, recv0, send1p, recv1p, send1q, recv1q, send2p, recv2p, send2q, recv2q, send3, recv3,
     grad, squares, full, send_sem, recv_sem, out_sem,
 ):
     gx, gy, gxx = sizes
@@ -89,10 +89,28 @@
 
     lane_p, lane_q = pl.ds(0, LANES), pl.ds(LANES, LANES)
 
-    core_in = [
-        copies.start(part.at[:, :, :, other, :, cols(k)], recv0.at[k], partner)
-        for k in range(chunks)
-    ]
+    core_in = {}
+    span = max(rows, 2 * LANES)
+
+    def stage0(k):
+        right = cotangents[:, cols(k)]
+
+        def body(b, _):
+            here = pl.ds(pl.multiple_of(b * span, span), span)
+            if k == 0:
+                left = tokens[:, here].T
+                flipped[here, :] = left
+            else:
+                left = flipped[here, :]
+            product = jnp.dot(left, right, preferred_element_type=f32).astype(bf16)
+            for e in range(span // rows):
+                d = b * (span // rows) + e
+                i, j, l = d // (gy * gz), lax.rem(d // gz, gy), lax.rem(d, gz) // 2
+                part[i, j, l, lax.rem(d, 2), :, cols(k)] = product[e * rows : (e + 1) * rows]
+            return 0
+
+        lax.fori_loop(0, tokens.shape[1] // span, body, 0)
+        core_in[k] = copies.start(part.at[:, :, :, other, :, cols(k)], recv0.at[k], partner)
 
     def pair(k, i, j, l, col, lane):
         return part[i, j, l, core, :, col].astype(f32) + recv0[k, i, j, l, :, lane].astype(f32)
@@ -195,7 +213,10 @@
         return total
 
     total = jnp.zeros((8, LANES), f32)
+    stage0(0)
     for t in range(chunks + 3):
+        if t + 1 < chunks:
+            stage0(t + 1)
         if t < chunks:
             stage1(t)
         if 0 <= t - 1 < chunks:
@@ -298,9 +319,6 @@
     chunks = columns // (2 * LANES)
     clip_norm = math.sqrt(width * columns)
     f32, bf16 = jnp.float32, jnp.bfloat16
-    partial = lax.dot_general(
-        tokens, cotangents, (((0,), (0,)), ((), ())), preferred_element_type=f32
-    ).astype(bf16)
     whole = (gx, gy, gxx, 2, rows, columns)
     per_chunk = (1 + 2 * ((gxx - 1) + (gy - 1)) + (gx - 1)) * 2
     count = chunks * per_chunk + gx + gy + 2 * gxx - 3
@@ -314,9 +332,11 @@
     weights, new_master, new_first, new_second = pl.pallas_call(
         functools.partial(kernel, sizes, chunks, clip_norm),
         out_shape=(jax.ShapeDtypeStruct(whole, bf16), state, state, state),
-        in_specs=[vmem] * 4,
+        in_specs=[vmem] * 5,
         out_specs=(pl.BlockSpec(memory_space=pl.ANY), vmem, vmem, vmem),
         scratch_shapes=[
+            pltpu.VMEM((width, tokens.shape[0]), bf16),
+            pltpu.VMEM(whole, bf16),
             pltpu.VMEM((chunks, gx, gy, gxx, rows, 2 * LANES), bf16),
             *twice(gxx - 1, gx, gy, *block),
             *twice(gy - 1, gx, gxx, *block),
@@ -331,9 +351,9 @@
             pltpu.SemaphoreType.DMA((2 * chunks,)),
         ],
         compiler_params=pltpu.CompilerParams(
-            collective_id=0, has_side_effects=True, vmem_limit_bytes=48 * 1024 * 1024
+            collective_id=0, has_side_effects=True, vmem_limit_bytes=56 * 1024 * 1024
         ),
-    )(partial.reshape(whole), master, first_moment, second_moment)
+    )(tokens, cotangents, master, first_moment, second_moment)
     return (weights.reshape(width, columns), new_master, new_first, new_second)
 
 

time: 148 us -> 142 us (0.959)
  matrix products: 14.6 us -> 0 us
  Pallas kernels: 121 us -> 131 us
    dot_general x1 -> x0, matrix products: 14.6 us -> none  [shards(): lax.dot_general(tokens, cotangents, (((0,), (0,)), ((), ())), preferred_e...]
    pallas_call x1, Pallas kernels: 121 us -> 131 us  [shards(): pl.pallas_call(functools.partial(kernel, sizes, chunks, clip_norm), out_s...]
    unnamed x12 -> x10, local copies, waits for them, and re-layouts: 11.7 us -> 10.3 us
where the time goes in v2:
time: 142 us
  Pallas kernels  131 us (92%)
  local copies, waits for them, and re-layouts  10.3 us (7%)
    pallas_call x1, Pallas kernels, shards(): pl.pallas_call(functools.partial(kernel, sizes, chunks, clip_norm), out_s...  131 us
    unnamed x10, local copies, waits for them, and re-layouts  10.3 us

profile of v2, /device:TPU:9, one launch (start us, length us, event | category | flops | bytes accessed | tf_op | source)
XLA Modules:
  0.0 142.0 jit_solution(4909703436125067023)
XLA Ops:
  0.6 131.1 %shard_map.84 = (bf16[4,2,2,2,128,1024]{5,4,3,2,1,0:T(8,128)(2,1)}, f32[128,1024]{1,0:T(8,128)}, f32[128,1024]{1,0:T(8,128)}, f32[128,1024]{1,0:T(8,128)}) custom-call(bf16[1024,4096]{1,0:T(8,128)(2,1)} %tokens.1, bf16[1024,1024]{1,0:T(8,128)(2,1)} %cotangents.1, f32[128,1024]{1,0:T(8,128)} %master.1, f32[128,1024]{1,0:T(8,128)} %first.1, f32[128,1024]{1,0:T(8,128)} %second.1), custom_call_target="tpu_custom_call" | custom-call | tf_op jit(solution)/shard_map/pallas_call | solution.py:332
  131.7 0.0 copy-start.2
  131.7 0.0 copy-start.1
  131.8 0.0 copy-start
  131.8 7.9 %copy.13 = bf16[4096,1024]{1,0:T(8,128)(2,1)} copy(bf16[4096,1024]{1,0:T(8,128)(2,1)} %bitcast.1) | data formatting | bytes 16777216
  139.6 0.0 copy-done.2
  139.6 0.8 copy.14
  140.4 0.0 copy-done.1
  140.4 0.8 copy.15
  141.2 0.0 copy-done
  141.2 0.8 copy.16
Async XLA Ops:
  131.7 7.9 %copy-start.2 = (f32[128,1024]{1,0:T(8,128)S(1)}, f32[128,1024]{1,0:T(8,128)}, u32[]{:S(2)}) copy-start(f32[128,1024]{1,0:T(8,128)} %get-tuple-element.17) | copy-start | bytes 1572868
  131.7 8.7 %copy-start.1 = (f32[128,1024]{1,0:T(8,128)S(1)}, f32[128,1024]{1,0:T(8,128)}, u32[]{:S(2)}) copy-start(f32[128,1024]{1,0:T(8,128)} %get-tuple-element.18) | copy-start | bytes 1572868
  131.8 9.5 %copy-start = (f32[128,1024]{1,0:T(8,128)S(1)}, f32[128,1024]{1,0:T(8,128)}, u32[]{:S(2)}) copy-start(f32[128,1024]{1,0:T(8,128)} %get-tuple-element.19) | copy-start | bytes 1572868
